TPU v7x, 128 devices: a whole 4x4x4 slice. The times are simulated.
128 devices in a mesh: seq: 8 (over x, z_lo), blk: 8 (over y, core), uly: 2 (over z_hi).
Axes of the slice: x: 4, y: 4, z: 4 (z_hi: 2, z_lo: 2; z = z_hi * 2 + z_lo), core: 2. Of those that a mesh axis runs over, the one named last changes fastest.
Arguments:
- queries: bfloat16 [32768, 5120], P(('seq', 'blk', 'uly')), parts along dimension 0, may hold values from -60 to 60, as said below
- keys: bfloat16 [32768, 1024], P(('seq', 'blk', 'uly')), parts along dimension 0, may hold values from -60 to 60, as said below
- values: bfloat16 [32768, 1024], P(('seq', 'blk', 'uly')), parts along dimension 0, may hold values from -6 to 6
- positions: int32 [3, 32768], P(None, ('seq', 'blk', 'uly')), parts along dimension 1, may hold values from 0 to 1038
- doc_lengths: int32 [64], P('seq'), parts along dimension 0, may hold values from 1 to 2048, 4096 in all
Outputs:
- attended: bfloat16 [32768, 5120], P(('seq', 'blk', 'uly')), parts along dimension 0
There are 8 independent parts, one for each index of `seq`. A program takes and returns all parts, laid end to end along the dimension named above; each array names one. Nothing has to cross between parts.
Inputs may be any that keep to these rules, and one draw needn't show every extreme that they name: queries; the query rows hold values of order one, a few rows may be much larger. keys; the key rows hold values of order one, a few rows may be much larger.
All inputs are finite; a program needn't handle non-finite values.
Results may differ from a plain program's by a relative error of at most 0.0055.
Values may be sent and summed in bfloat16 or wider, within the bound.
A program may use at most 384 MiB of HBM per device.

v0:
```python
import math

import jax
import jax.numpy as jnp
from jax import lax
from jax.sharding import PartitionSpec as P

HEAD_SIZE = 128
QUERY_PER_KEY = 5


def apply_rotary(x, pos, heads):
    rows = x.shape[0]
    half = HEAD_SIZE // 2
    pair = jnp.arange(half, dtype=jnp.int32)
    freq = jnp.power(jnp.float32(1000000.0), -2.0 * pair.astype(jnp.float32) / HEAD_SIZE)
    place = pos.astype(jnp.float32)
    first = HEAD_SIZE // 8
    second = first + 3 * HEAD_SIZE // 16
    chosen = jnp.where(
        pair[None, :] < first,
        place[0][:, None],
        jnp.where(pair[None, :] < second, place[1][:, None], place[2][:, None]),
    )
    angle = chosen * freq[None, :]
    cosine = jnp.cos(angle)[:, None, :]
    sine = jnp.sin(angle)[:, None, :]
    parts = x.reshape(rows, heads, HEAD_SIZE).astype(jnp.float32)
    lower = parts[..., :half]
    upper = parts[..., half:]
    turned = jnp.concatenate(
        [lower * cosine - upper * sine, upper * cosine + lower * sine], axis=-1
    )
    return turned.reshape(rows, heads * HEAD_SIZE).astype(jnp.bfloat16)


def doc_starts(index, doc_lengths):
    ends = jnp.cumsum(doc_lengths)
    return jnp.sum(jnp.where(ends[None, :] <= index[:, None], doc_lengths[None, :], 0), axis=1)


def attend(rotated, query_index, query_start, kheads, folder):
    rows = rotated.shape[0]
    scale = 1.0 / math.sqrt(HEAD_SIZE)
    grouped_query = rotated.reshape(rows, kheads, QUERY_PER_KEY, HEAD_SIZE)
    last_query = query_index[rows - 1]
    first_start = jnp.min(query_start)

    def update(carry, keys_blk, values_blk, begin):
        best, total, summed = carry
        width = keys_blk.shape[0]
        key_index = begin + jnp.arange(width, dtype=jnp.int32)
        allowed = (key_index[None, :] <= query_index[:, None]) & (
            key_index[None, :] >= query_start[:, None]
        )
        scores = (
            jnp.einsum(
                "rhgd,bhd->hgrb", grouped_query, keys_blk, preferred_element_type=jnp.float32
            )
            * scale
        )
        scores = jnp.where(allowed, scores, -1e30)
        newbest = jnp.maximum(best, jnp.max(scores, axis=-1))
        weights = jnp.where(allowed, jnp.exp(scores - newbest[..., None]), 0.0)
        factor = jnp.exp(best - newbest)
        total = total * factor + jnp.sum(weights, axis=-1)
        summed = summed * factor[..., None] + jnp.einsum(
            "hgrb,bhd->hgrd",
            weights.astype(jnp.bfloat16),
            values_blk,
            preferred_element_type=jnp.float32,
        )
        return (newbest, total, summed)

    def fold_piece(carry, piece, start):
        count = piece.shape[0]
        block = math.gcd(count, 512)

        def step(turn, inner):
            offset = turn * block
            slab = lax.dynamic_slice_in_dim(piece, offset, block, 0)
            keys_blk = slab[:, : kheads * HEAD_SIZE].reshape(block, kheads, HEAD_SIZE)
            values_blk = slab[:, kheads * HEAD_SIZE :].reshape(block, kheads, HEAD_SIZE)
            live = (offset <= last_query) & (offset + block - 1 >= first_start)

            def taken(state):
                return update(state, keys_blk, values_blk, offset)

            def passed(state):
                return state

            return lax.cond(live, taken, passed, inner)

        return lax.fori_loop(0, count // block, step, carry)

    initial = (
        jnp.full((kheads, QUERY_PER_KEY, rows), -1e30, jnp.float32),
        jnp.zeros((kheads, QUERY_PER_KEY, rows), jnp.float32),
        jnp.zeros((kheads, QUERY_PER_KEY, rows, HEAD_SIZE), jnp.float32),
    )
    best, total, summed = folder(fold_piece, initial)
    result = summed / total[..., None]
    return (
        jnp.transpose(result, (2, 0, 1, 3))
        .reshape(rows, kheads * QUERY_PER_KEY * HEAD_SIZE)
        .astype(jnp.bfloat16)
    )


def local(queries, keys, values, positions, doc_lengths):
    rows = queries.shape[0]
    kheads = keys.shape[1] // HEAD_SIZE
    query_rotated = apply_rotary(queries, positions, queries.shape[1] // HEAD_SIZE)
    key_rotated = apply_rotary(keys, positions, kheads)
    index = lax.axis_index(("blk", "uly")) * rows + jnp.arange(rows, dtype=jnp.int32)
    starts = doc_starts(index, doc_lengths)
    paired = jnp.concatenate([key_rotated, values], axis=1)

    def fold_all(fn, init):
        return fn(init, lax.all_gather(paired, ("blk", "uly"), axis=0, tiled=True), jnp.int32(0))

    return attend(query_rotated, index, starts, kheads, fold_all)


def solution(mesh):
    in_specs = (
        P(("seq", "blk", "uly"), None),
        P(("seq", "blk", "uly"), None),
        P(("seq", "blk", "uly"), None),
        P(None, ("seq", "blk", "uly")),
        P("seq"),
    )
    out_specs = P(("seq", "blk", "uly"), None)
    return jax.shard_map(local, mesh=mesh, in_specs=in_specs, out_specs=out_specs, check_vma=False)
```

profile of v0, /device:TPU:28, one launch (start us, length us, event | category | flops | bytes accessed | tf_op | source)
XLA Modules:
  0.0 311.9 jit_solution(8783255443891443507)
XLA Ops:
  6.6 0.7 convert_element_type.62
  7.3 0.6 fusion.14
  8.0 1.2 copy.29
  9.3 1.2 copy.41
  10.7 1.1 pad_maximum_fusion.1
  11.9 0.6 slice.49
  12.8 0.6 convert_bitcast_fusion
  13.4 3.2 %copy.44 = f32[32,8,40,128]{3,2,1,0:T(8,128)} copy(f32[32,8,40,128]{3,1,2,0:T(8,128)S(1)} %convert_bitcast_fusion) | data formatting | bytes 10485760
  16.9 0.7 reduce_min.9
  17.6 5.7 %fusion.16 = (f32[256,40,64]{2,1,0:T(8,128)S(1)}, f32[256,40,64]{2,1,0:T(8,128)S(1)}) fusion(f32[256,40,128]{2,1,0:T(8,128)} %bitcast.43), kind=kLoop, calls=%fused_computation.36 | loop fusion | bytes 10485760 | tf_op jit(solution)/shard_map/slice | solution.py:29
  23.3 2.1 subtract_convert_fusion
  25.5 2.9 pad_maximum_fusion
  28.4 106.9 %all-gather.2.cloned.1.call-done = bf16[4096,2048]{0,1:T(8,128)(2,1)} async-done(((bf16[256,2048]{0,1:T(8,128)(2,1)}), bf16[4096,2048]{0,1:T(8,128)(2,1)}) %all-gather.2.cloned.1.call-update) | async-done | bytes 16777232 | tf_op jit(solution)/shard_map/all_gather | solution.py:120
  135.3 2.9 broadcast_in_dim.122
  138.2 155.0 %while.22 = (s32[]{:T(128)}, f32[8,5,256]{2,1,0:T(8,128)S(1)}, f32[8,5,256]{2,1,0:T(8,128)S(1)}, f32[8,5,256,128]{3,2,1,0:T(8,128)}, s32[]{:T(128)}, /*index=5*/...) while((s32[]{:T(128)}, f32[8,5,256]{2,1,0:T(8,128)S(1)}, ...), condition=%wide.region_8.9_spmd.clone, body=%wide.region_3.8_spmd.clone.sunk | while | flops 2755547904 | bytes 171582896 | solution.py:94
  141.9 29.0 %conditional.3 = ((f32[8,5,256]{2,1,0:T(8,128)S(1)}, f32[8,5,256]{2,1,0:T(8,128)S(1)}, f32[8,5,256,128]{3,2,1,0:T(8,128)})) conditional(s32[]{:T(128)} %convert_element_type.82, (f32[8,5,256]{2,1,0:T(8,128)S(1)}, f32[8,5,256]{2,1,0:T(8,128)S(1)}, f32[8,5,256,128]{3,2,1,0:T(8,128)}) %tuple.77, (s32[]{:T(128)}, s32[]{:T(128)}, s32[256]{0:T(256)S(1)}, ...), branch_computations={%region_4.4_spmd, %region_5.7_spmd} | conditional | flops 2755547904 | bytes 171581600 | solution.py:92
  142.1 2.7 fusion.15
  144.9 5.1 %fusion.2 = (f32[8,5,256]{2,1,0:T(8,128)S(1)}, f32[8,512,256,5]{2,1,3,0:T(8,128)S(1)}) fusion(pred[256,512]{0,1:T(8,128)(4,1)S(1)} %compare_and_fusion, bf16[512,8,128,1]{0,2,3,1:T(8,128)(2,1)S(1)} %bitcast.42, bf16[256,8,5,128]{3,0,2,1:T(8,128)(2,1)} %get-tuple-element.418), kind=kOutput, calls=%fused_computation.3 | convolution fusion | flops 1357895680 | bytes 24813568 | tf_op jit(solution)/shard_map/while/body/eval_jaxpr/cond/branch_1_fun/rhgd,bhd->hgrb/dot_general | solution.py:57
  150.0 5.0 %fusion.4 = f32[8,5,256]{2,1,0:T(8,128)S(1)} fusion(f32[8,512,256,5]{2,1,3,0:T(8,128)S(1)} %get-tuple-element.493, f32[8,5,256]{2,1,0:T(8,128)S(1)} %max.4, pred[256,512]{0,1:T(8,128)(4,1)S(1)} %compare_and_fusion), kind=kLoop, calls=%fused_computation.5 | loop fusion | flops 26204160 | bytes 21184512 | tf_op jit(solution)/shard_map/while/body/eval_jaxpr/cond/branch_1_fun/reduce_sum | solution.py:66
  155.1 2.2 copy-done
  157.3 13.6 %multiply_add_fusion = f32[8,5,256,128]{3,2,1,0:T(8,128)} fusion(f32[8,5,256,128]{3,2,1,0:T(8,128)} %get-tuple-element.420, f32[8,5,256]{2,1,0:T(8,128)S(1)} %get-tuple-element.489, bf16[512,8,128,1]{0,2,3,1:T(8,128)(2,1)S(1)} %bitcast.44, f32[8,512,256,5]{2,1,3,0:T(8,128)} %copy-done, f32[8,5,256]{2,1,0:T(8,128)S(1)} %max.4, ...), kind=kOutput, calls=%fused_computation.8 | convolution fusion | flops 1371013120 | bytes 32718848 | tf_op jit(solution)/shard_map/while/body/eval_jaxpr/cond/branch_1_fun/hgrb,bhd->hgrd/dot_general | solution.py:67
  172.2 29.0 %conditional.3 = ((f32[8,5,256]{2,1,0:T(8,128)S(1)}, f32[8,5,256]{2,1,0:T(8,128)S(1)}, f32[8,5,256,128]{3,2,1,0:T(8,128)})) conditional(s32[]{:T(128)} %convert_element_type.82, (f32[8,5,256]{2,1,0:T(8,128)S(1)}, f32[8,5,256]{2,1,0:T(8,128)S(1)}, f32[8,5,256,128]{3,2,1,0:T(8,128)}) %tuple.77, (s32[]{:T(128)}, s32[]{:T(128)}, s32[256]{0:T(256)S(1)}, ...), branch_computations={%region_4.4_spmd, %region_5.7_spmd} | conditional | flops 2755547904 | bytes 171581600 | solution.py:92
  172.4 2.7 fusion.15
  175.1 5.1 %fusion.2 = (f32[8,5,256]{2,1,0:T(8,128)S(1)}, f32[8,512,256,5]{2,1,3,0:T(8,128)S(1)}) fusion(pred[256,512]{0,1:T(8,128)(4,1)S(1)} %compare_and_fusion, bf16[512,8,128,1]{0,2,3,1:T(8,128)(2,1)S(1)} %bitcast.42, bf16[256,8,5,128]{3,0,2,1:T(8,128)(2,1)} %get-tuple-element.418), kind=kOutput, calls=%fused_computation.3 | convolution fusion | flops 1357895680 | bytes 24813568 | tf_op jit(solution)/shard_map/while/body/eval_jaxpr/cond/branch_1_fun/rhgd,bhd->hgrb/dot_general | solution.py:57
  180.3 5.0 %fusion.4 = f32[8,5,256]{2,1,0:T(8,128)S(1)} fusion(f32[8,512,256,5]{2,1,3,0:T(8,128)S(1)} %get-tuple-element.493, f32[8,5,256]{2,1,0:T(8,128)S(1)} %max.4, pred[256,512]{0,1:T(8,128)(4,1)S(1)} %compare_and_fusion), kind=kLoop, calls=%fused_computation.5 | loop fusion | flops 26204160 | bytes 21184512 | tf_op jit(solution)/shard_map/while/body/eval_jaxpr/cond/branch_1_fun/reduce_sum | solution.py:66
  185.3 2.2 copy-done
  187.6 13.6 %multiply_add_fusion = f32[8,5,256,128]{3,2,1,0:T(8,128)} fusion(f32[8,5,256,128]{3,2,1,0:T(8,128)} %get-tuple-element.420, f32[8,5,256]{2,1,0:T(8,128)S(1)} %get-tuple-element.489, bf16[512,8,128,1]{0,2,3,1:T(8,128)(2,1)S(1)} %bitcast.44, f32[8,512,256,5]{2,1,3,0:T(8,128)} %copy-done, f32[8,5,256]{2,1,0:T(8,128)S(1)} %max.4, ...), kind=kOutput, calls=%fused_computation.8 | convolution fusion | flops 1371013120 | bytes 32718848 | tf_op jit(solution)/shard_map/while/body/eval_jaxpr/cond/branch_1_fun/hgrb,bhd->hgrd/dot_general | solution.py:67
  202.4 29.0 %conditional.3 = ((f32[8,5,256]{2,1,0:T(8,128)S(1)}, f32[8,5,256]{2,1,0:T(8,128)S(1)}, f32[8,5,256,128]{3,2,1,0:T(8,128)})) conditional(s32[]{:T(128)} %convert_element_type.82, (f32[8,5,256]{2,1,0:T(8,128)S(1)}, f32[8,5,256]{2,1,0:T(8,128)S(1)}, f32[8,5,256,128]{3,2,1,0:T(8,128)}) %tuple.77, (s32[]{:T(128)}, s32[]{:T(128)}, s32[256]{0:T(256)S(1)}, ...), branch_computations={%region_4.4_spmd, %region_5.7_spmd} | conditional | flops 2755547904 | bytes 171581600 | solution.py:92
  202.6 2.7 fusion.15
  205.4 5.1 %fusion.2 = (f32[8,5,256]{2,1,0:T(8,128)S(1)}, f32[8,512,256,5]{2,1,3,0:T(8,128)S(1)}) fusion(pred[256,512]{0,1:T(8,128)(4,1)S(1)} %compare_and_fusion, bf16[512,8,128,1]{0,2,3,1:T(8,128)(2,1)S(1)} %bitcast.42, bf16[256,8,5,128]{3,0,2,1:T(8,128)(2,1)} %get-tuple-element.418), kind=kOutput, calls=%fused_computation.3 | convolution fusion | flops 1357895680 | bytes 24813568 | tf_op jit(solution)/shard_map/while/body/eval_jaxpr/cond/branch_1_fun/rhgd,bhd->hgrb/dot_general | solution.py:57
  210.5 5.0 %fusion.4 = f32[8,5,256]{2,1,0:T(8,128)S(1)} fusion(f32[8,512,256,5]{2,1,3,0:T(8,128)S(1)} %get-tuple-element.493, f32[8,5,256]{2,1,0:T(8,128)S(1)} %max.4, pred[256,512]{0,1:T(8,128)(4,1)S(1)} %compare_and_fusion), kind=kLoop, calls=%fused_computation.5 | loop fusion | flops 26204160 | bytes 21184512 | tf_op jit(solution)/shard_map/while/body/eval_jaxpr/cond/branch_1_fun/reduce_sum | solution.py:66
  215.6 2.2 copy-done
  217.8 13.6 %multiply_add_fusion = f32[8,5,256,128]{3,2,1,0:T(8,128)} fusion(f32[8,5,256,128]{3,2,1,0:T(8,128)} %get-tuple-element.420, f32[8,5,256]{2,1,0:T(8,128)S(1)} %get-tuple-element.489, bf16[512,8,128,1]{0,2,3,1:T(8,128)(2,1)S(1)} %bitcast.44, f32[8,512,256,5]{2,1,3,0:T(8,128)} %copy-done, f32[8,5,256]{2,1,0:T(8,128)S(1)} %max.4, ...), kind=kOutput, calls=%fused_computation.8 | convolution fusion | flops 1371013120 | bytes 32718848 | tf_op jit(solution)/shard_map/while/body/eval_jaxpr/cond/branch_1_fun/hgrb,bhd->hgrd/dot_general | solution.py:67
  232.7 29.0 %conditional.3 = ((f32[8,5,256]{2,1,0:T(8,128)S(1)}, f32[8,5,256]{2,1,0:T(8,128)S(1)}, f32[8,5,256,128]{3,2,1,0:T(8,128)})) conditional(s32[]{:T(128)} %convert_element_type.82, (f32[8,5,256]{2,1,0:T(8,128)S(1)}, f32[8,5,256]{2,1,0:T(8,128)S(1)}, f32[8,5,256,128]{3,2,1,0:T(8,128)}) %tuple.77, (s32[]{:T(128)}, s32[]{:T(128)}, s32[256]{0:T(256)S(1)}, ...), branch_computations={%region_4.4_spmd, %region_5.7_spmd} | conditional | flops 2755547904 | bytes 171581600 | solution.py:92
  232.9 2.7 fusion.15
  235.6 5.1 %fusion.2 = (f32[8,5,256]{2,1,0:T(8,128)S(1)}, f32[8,512,256,5]{2,1,3,0:T(8,128)S(1)}) fusion(pred[256,512]{0,1:T(8,128)(4,1)S(1)} %compare_and_fusion, bf16[512,8,128,1]{0,2,3,1:T(8,128)(2,1)S(1)} %bitcast.42, bf16[256,8,5,128]{3,0,2,1:T(8,128)(2,1)} %get-tuple-element.418), kind=kOutput, calls=%fused_computation.3 | convolution fusion | flops 1357895680 | bytes 24813568 | tf_op jit(solution)/shard_map/while/body/eval_jaxpr/cond/branch_1_fun/rhgd,bhd->hgrb/dot_general | solution.py:57
  240.8 5.0 %fusion.4 = f32[8,5,256]{2,1,0:T(8,128)S(1)} fusion(f32[8,512,256,5]{2,1,3,0:T(8,128)S(1)} %get-tuple-element.493, f32[8,5,256]{2,1,0:T(8,128)S(1)} %max.4, pred[256,512]{0,1:T(8,128)(4,1)S(1)} %compare_and_fusion), kind=kLoop, calls=%fused_computation.5 | loop fusion | flops 26204160 | bytes 21184512 | tf_op jit(solution)/shard_map/while/body/eval_jaxpr/cond/branch_1_fun/reduce_sum | solution.py:66
  245.8 2.2 copy-done
  248.1 13.6 %multiply_add_fusion = f32[8,5,256,128]{3,2,1,0:T(8,128)} fusion(f32[8,5,256,128]{3,2,1,0:T(8,128)} %get-tuple-element.420, f32[8,5,256]{2,1,0:T(8,128)S(1)} %get-tuple-element.489, bf16[512,8,128,1]{0,2,3,1:T(8,128)(2,1)S(1)} %bitcast.44, f32[8,512,256,5]{2,1,3,0:T(8,128)} %copy-done, f32[8,5,256]{2,1,0:T(8,128)S(1)} %max.4, ...), kind=kOutput, calls=%fused_computation.8 | convolution fusion | flops 1371013120 | bytes 32718848 | tf_op jit(solution)/shard_map/while/body/eval_jaxpr/cond/branch_1_fun/hgrb,bhd->hgrd/dot_general | solution.py:67
  262.9 29.0 %conditional.3 = ((f32[8,5,256]{2,1,0:T(8,128)S(1)}, f32[8,5,256]{2,1,0:T(8,128)S(1)}, f32[8,5,256,128]{3,2,1,0:T(8,128)})) conditional(s32[]{:T(128)} %convert_element_type.82, (f32[8,5,256]{2,1,0:T(8,128)S(1)}, f32[8,5,256]{2,1,0:T(8,128)S(1)}, f32[8,5,256,128]{3,2,1,0:T(8,128)}) %tuple.77, (s32[]{:T(128)}, s32[]{:T(128)}, s32[256]{0:T(256)S(1)}, ...), branch_computations={%region_4.4_spmd, %region_5.7_spmd} | conditional | flops 2755547904 | bytes 171581600 | solution.py:92
  263.2 2.7 fusion.15
  265.9 5.1 %fusion.2 = (f32[8,5,256]{2,1,0:T(8,128)S(1)}, f32[8,512,256,5]{2,1,3,0:T(8,128)S(1)}) fusion(pred[256,512]{0,1:T(8,128)(4,1)S(1)} %compare_and_fusion, bf16[512,8,128,1]{0,2,3,1:T(8,128)(2,1)S(1)} %bitcast.42, bf16[256,8,5,128]{3,0,2,1:T(8,128)(2,1)} %get-tuple-element.418), kind=kOutput, calls=%fused_computation.3 | convolution fusion | flops 1357895680 | bytes 24813568 | tf_op jit(solution)/shard_map/while/body/eval_jaxpr/cond/branch_1_fun/rhgd,bhd->hgrb/dot_general | solution.py:57
  271.0 5.0 %fusion.4 = f32[8,5,256]{2,1,0:T(8,128)S(1)} fusion(f32[8,512,256,5]{2,1,3,0:T(8,128)S(1)} %get-tuple-element.493, f32[8,5,256]{2,1,0:T(8,128)S(1)} %max.4, pred[256,512]{0,1:T(8,128)(4,1)S(1)} %compare_and_fusion), kind=kLoop, calls=%fused_computation.5 | loop fusion | flops 26204160 | bytes 21184512 | tf_op jit(solution)/shard_map/while/body/eval_jaxpr/cond/branch_1_fun/reduce_sum | solution.py:66
  276.1 2.2 copy-done
  278.4 13.6 %multiply_add_fusion = f32[8,5,256,128]{3,2,1,0:T(8,128)} fusion(f32[8,5,256,128]{3,2,1,0:T(8,128)} %get-tuple-element.420, f32[8,5,256]{2,1,0:T(8,128)S(1)} %get-tuple-element.489, bf16[512,8,128,1]{0,2,3,1:T(8,128)(2,1)S(1)} %bitcast.44, f32[8,512,256,5]{2,1,3,0:T(8,128)} %copy-done, f32[8,5,256]{2,1,0:T(8,128)S(1)} %max.4, ...), kind=kOutput, calls=%fused_computation.8 | convolution fusion | flops 1371013120 | bytes 32718848 | tf_op jit(solution)/shard_map/while/body/eval_jaxpr/cond/branch_1_fun/hgrb,bhd->hgrd/dot_general | solution.py:67
  293.2 5.9 %copy.32 = f32[8,5,256,128]{2,3,1,0:T(8,128)} copy(f32[8,5,256,128]{3,2,1,0:T(8,128)} %get-tuple-element.437) | data formatting | bytes 10485760 | tf_op jit(solution)/shard_map/while | solution.py:94
  299.1 3.1 %divide_convert_fusion = bf16[8,5,256,128]{2,3,1,0:T(8,128)(2,1)S(1)} fusion(f32[8,5,256,128]{2,3,1,0:T(8,128)} %copy.32, f32[8,5,256]{2,1,0:T(8,128)S(1)} %get-tuple-element.438), kind=kLoop, calls=%fused_computation.19 | loop fusion | flops 2621440 | bytes 7905280 | tf_op jit(solution)/shard_map/convert_element_type | solution.py:106
  302.3 2.8 copy.33
  (74 shorter events, 2.3 us)
Async XLA Ops:
  6.5 128.8 %all-gather.2.cloned.1.call-start = ((), (), s32[]{:S(2)}) async-start(), calls=%async_computation | async-start | bytes 17825792 | tf_op jit(solution)/shard_map/all_gather | solution.py:120
  10.7 2.1 copy-start.2
  13.4 3.2 %copy-start.3 = (s32[8]{0:T(128)S(1)}, s32[8]{0:T(128)}, u32[]{:S(2)}) copy-start(s32[8]{0:T(128)} %param.13) | copy-start | bytes 100
  150.0 7.3 %copy-start = (f32[8,512,256,5]{2,1,3,0:T(8,128)}, f32[8,512,256,5]{2,1,3,0:T(8,128)S(1)}, u32[]{:S(2)}) copy-start(f32[8,512,256,5]{2,1,3,0:T(8,128)S(1)} %get-tuple-element.493) | copy-start | bytes 62914564 | tf_op jit(solution)/shard_map/while/body/eval_jaxpr/cond
  150.0 7.3 %copy-start.1 = (bf16[512,1024]{0,1:T(8,128)(2,1)S(1)}, bf16[512,1024]{0,1:T(8,128)(2,1)}, u32[]{:S(2)}) copy-start(bf16[512,1024]{0,1:T(8,128)(2,1)} %get-tuple-element.490) | copy-start | bytes 3145732 | tf_op jit(solution)/shard_map/while/body/eval_jaxpr/cond
  180.2 7.3 %copy-start = (f32[8,512,256,5]{2,1,3,0:T(8,128)}, f32[8,512,256,5]{2,1,3,0:T(8,128)S(1)}, u32[]{:S(2)}) copy-start(f32[8,512,256,5]{2,1,3,0:T(8,128)S(1)} %get-tuple-element.493) | copy-start | bytes 62914564 | tf_op jit(solution)/shard_map/while/body/eval_jaxpr/cond
  180.3 7.3 %copy-start.1 = (bf16[512,1024]{0,1:T(8,128)(2,1)S(1)}, bf16[512,1024]{0,1:T(8,128)(2,1)}, u32[]{:S(2)}) copy-start(bf16[512,1024]{0,1:T(8,128)(2,1)} %get-tuple-element.490) | copy-start | bytes 3145732 | tf_op jit(solution)/shard_map/while/body/eval_jaxpr/cond
  210.5 7.3 %copy-start = (f32[8,512,256,5]{2,1,3,0:T(8,128)}, f32[8,512,256,5]{2,1,3,0:T(8,128)S(1)}, u32[]{:S(2)}) copy-start(f32[8,512,256,5]{2,1,3,0:T(8,128)S(1)} %get-tuple-element.493) | copy-start | bytes 62914564 | tf_op jit(solution)/shard_map/while/body/eval_jaxpr/cond
  210.5 7.3 %copy-start.1 = (bf16[512,1024]{0,1:T(8,128)(2,1)S(1)}, bf16[512,1024]{0,1:T(8,128)(2,1)}, u32[]{:S(2)}) copy-start(bf16[512,1024]{0,1:T(8,128)(2,1)} %get-tuple-element.490) | copy-start | bytes 3145732 | tf_op jit(solution)/shard_map/while/body/eval_jaxpr/cond
  240.7 7.3 %copy-start = (f32[8,512,256,5]{2,1,3,0:T(8,128)}, f32[8,512,256,5]{2,1,3,0:T(8,128)S(1)}, u32[]{:S(2)}) copy-start(f32[8,512,256,5]{2,1,3,0:T(8,128)S(1)} %get-tuple-element.493) | copy-start | bytes 62914564 | tf_op jit(solution)/shard_map/while/body/eval_jaxpr/cond
  240.8 7.3 %copy-start.1 = (bf16[512,1024]{0,1:T(8,128)(2,1)S(1)}, bf16[512,1024]{0,1:T(8,128)(2,1)}, u32[]{:S(2)}) copy-start(bf16[512,1024]{0,1:T(8,128)(2,1)} %get-tuple-element.490) | copy-start | bytes 3145732 | tf_op jit(solution)/shard_map/while/body/eval_jaxpr/cond
  271.0 7.3 %copy-start = (f32[8,512,256,5]{2,1,3,0:T(8,128)}, f32[8,512,256,5]{2,1,3,0:T(8,128)S(1)}, u32[]{:S(2)}) copy-start(f32[8,512,256,5]{2,1,3,0:T(8,128)S(1)} %get-tuple-element.493) | copy-start | bytes 62914564 | tf_op jit(solution)/shard_map/while/body/eval_jaxpr/cond
  271.0 7.3 %copy-start.1 = (bf16[512,1024]{0,1:T(8,128)(2,1)S(1)}, bf16[512,1024]{0,1:T(8,128)(2,1)}, u32[]{:S(2)}) copy-start(bf16[512,1024]{0,1:T(8,128)(2,1)} %get-tuple-element.490) | copy-start | bytes 3145732 | tf_op jit(solution)/shard_map/while/body/eval_jaxpr/cond
Sparse Core Ops, SparseCore 0:
  12.0 123.3 all-gather.1
where the time goes:
time: 313 us; the launch traced here: 312 us
  waiting for transfers between devices  107 us (34%)
  matrix products  93.6 us (30%)
  local copies, waits for them, and re-layouts  48.9 us (16%)
  other arithmetic  38.7 us (12%)
  between operations  13.5 us (4%)
  loops' own time  10.3 us (3%)
    all_gather x1, waiting for transfers between devices, fold_all(): lax.all_gather(paired, ('blk', 'uly'), axis=0, tiled=True)  107 us
    dot_general x5, matrix products, update(): jnp.einsum('hgrb,bhd->hgrd', weights.astype(jnp.bfloat16), values_blk, pr...  68 us
    dot_general x5, matrix products, update(): jnp.einsum('rhgd,bhd->hgrb', grouped_query, keys_blk, preferred_element_t...  25.6 us
    reduce_sum x5, other arithmetic, update(): total = total * factor + jnp.sum(weights, axis=-1)  25.2 us
    slice x5, local copies, waits for them, and re-layouts, step(): values_blk = slab[:, kheads * HEAD_SIZE:].reshape(block, kheads, HEAD_SIZE)  13.6 us
    cond x25, local copies, waits for them, and re-layouts  11.1 us
    another operation x1, loops' own time, fold_piece(): return lax.fori_loop(0, count // block, step, carry)  9.73 us
  transfers between devices with their start and end apart: 1, of which 1 were waited for; matrix products, arithmetic and copies ran while one was open for 5% of the time, Pallas kernels for 0%

commit v1 on v0

v1 whole, which is shorter than its diff:
```python
import math

import jax
import jax.numpy as jnp
import numpy as np
from jax import lax
from jax.experimental import pallas as pl
from jax.experimental.pallas import tpu as pltpu
from jax.sharding import PartitionSpec as P

D = 128
G = 5
KH = 8
ROWS = 256
LAG = 2
HALF = D // 2
BIG = 3.0e38
LOW = -1.0e30
EXP_SCALE = math.log2(math.e) / math.sqrt(D)
MESH = pl.DeviceIdType.MESH
CONTRACT_LAST = (((1,), (1,)), ((), ()))
CONTRACT_FIRST = (((0,), (0,)), ((), ()))


def kernel(
    q_hbm, k_hbm, v_hbm, pos_ref, freq_ref, docs_ref, out_hbm,
    buf, qraw, qs, kraw, acc, best, total, masks, cos_t, sin_t, ostage,
    in_sem, v_sem, out_sem, send_sem, recv_sem,
):
    s = lax.axis_index("seq")
    blk = lax.axis_index("blk")
    z = lax.axis_index("uly")
    y = lax.div(blk, 2)
    c = lax.rem(blk, 2)
    own = 4 * y + 2 * c + z
    up = (s, 2 * lax.rem(y + 1, 4) + c, z)
    down = (s, 2 * lax.rem(y + 3, 4) + c, z)
    across = (s, blk, 1 - z)
    sibling = (s, 2 * y + 1 - c, z)
    links = (up, down, across, sibling)

    def slot(back, core, zz):
        return 4 * lax.rem(y + 4 - back, 4) + 2 * zz + core

    own_slot = slot(0, c, z)

    k_copy = pltpu.make_async_copy(k_hbm, kraw, in_sem.at[0])
    k_copy.start()
    v_copies = [
        pltpu.make_async_copy(
            v_hbm.at[:, h * D:(h + 1) * D], buf.at[own_slot, h, ROWS:2 * ROWS, :], v_sem.at[h]
        )
        for h in range(KH)
    ]
    for copy in v_copies:
        copy.start()
    q_copy = pltpu.make_async_copy(q_hbm, qraw, in_sem.at[1])
    q_copy.start()

    barrier = pltpu.get_barrier_semaphore()
    for peer in links:
        pl.semaphore_signal(barrier, inc=1, device_id=peer, device_id_type=MESH)

    pair = lax.broadcasted_iota(jnp.int32, (HALF, ROWS), 0)
    place = pos_ref[...].astype(jnp.float32)
    chosen = jnp.where(
        pair < D // 8,
        place[0:1, :],
        jnp.where(pair < D // 8 + 3 * D // 16, place[1:2, :], place[2:3, :]),
    )
    angle = chosen * freq_ref[...]
    cosine = jnp.cos(angle)
    sine = jnp.sin(angle)
    cos_t[...] = jnp.concatenate([cosine, cosine], axis=0).T
    sin_t[...] = jnp.concatenate([-sine, sine], axis=0).T

    def rotate(x):
        x = x.astype(jnp.float32)
        return (x * cos_t[...] + pltpu.roll(x, HALF, 1) * sin_t[...]).astype(jnp.bfloat16)

    k_copy.wait()
    for h in range(KH):
        buf[own_slot, h, 0:ROWS, :] = rotate(kraw[:, h * D:(h + 1) * D])
    for copy in v_copies:
        copy.wait()

    query_index = own * ROWS + lax.broadcasted_iota(jnp.int32, (1, ROWS), 1)
    start = jnp.zeros((1, ROWS), jnp.int32)
    end = 0
    for d in range(8):
        length = docs_ref[d]
        end = end + length
        start = start + jnp.where(query_index >= end, length, 0)
    key_row = lax.broadcasted_iota(jnp.int32, (2 * ROWS, ROWS), 0)
    key_row = key_row + jnp.where(key_row >= ROWS, ROWS, 0)
    for pair_at in range(6):
        back, flip = pair_at // 2, pair_at % 2
        zz = 1 - z if flip else z
        key_index = key_row + (4 * (y - back) + zz) * ROWS
        allowed = (key_index >= start) & (key_index <= query_index)
        masks[pair_at] = jnp.where(allowed, BIG, LOW)

    pl.semaphore_wait(barrier, 4)

    def send(link, block, h, count):
        return pltpu.make_async_remote_copy(
            src_ref=buf.at[block, h],
            dst_ref=buf.at[block, h],
            send_sem=send_sem.at[link * 16 + count],
            recv_sem=recv_sem.at[block * 8 + h],
            device_id=links[link],
            device_id_type=MESH,
        )

    def arrived(block, h):
        pltpu.make_async_copy(
            buf.at[block, h], buf.at[block, h], recv_sem.at[block * 8 + h]
        ).wait()

    @pl.loop(0, KH)
    def _(h):
        for link in range(4):
            send(link, own_slot, h, h).start()

    acc[...] = jnp.zeros_like(acc)
    total[...] = jnp.zeros_like(total)
    best[...] = jnp.full_like(best, LOW)
    q_copy.wait()

    @pl.loop(0, KH * G)
    def _(i):
        qs[i] = rotate(qraw[:, pl.ds(pl.multiple_of(i * D, D), D)])

    def update(keys, vals, mask, h):
        scores = [
            lax.dot_general(keys, qs[h * G + g], CONTRACT_LAST, preferred_element_type=jnp.float32)
            for g in range(G)
        ]
        olds = [best[h * G + g] for g in range(G)]
        sums = [total[h * G + g] for g in range(G)]
        news, factors, parts, weights = [], [], [], []
        for g in range(G):
            sc = jnp.minimum(scores[g], mask)
            new = jnp.maximum(olds[g], jnp.max(sc, axis=0, keepdims=True))
            w = jnp.exp2(sc * EXP_SCALE - new * EXP_SCALE)
            news.append(new)
            factors.append(jnp.exp2((olds[g] - new) * EXP_SCALE))
            parts.append(jnp.sum(w, axis=0, keepdims=True))
            weights.append(w.astype(jnp.bfloat16))
        outs = [
            lax.dot_general(vals, weights[g], CONTRACT_FIRST, preferred_element_type=jnp.float32)
            for g in range(G)
        ]
        for g in range(G):
            i = h * G + g
            best[i] = news[g]
            total[i] = sums[g] * factors[g] + parts[g]
            acc[i] = acc[i] * factors[g] + outs[g]

    def needed(back, core, zz):
        block = 4 * (y - back) + 2 * core + zz
        return (block >= 0) & (block >= own - 8) & (block <= own)

    def compute(u):
        phase = lax.div(jnp.minimum(u, 15), 8)
        late = u - 8 - LAG

        @pl.loop(0, 3)
        def _(j):
            back = jnp.where(phase == 0, jnp.where(j == 1, 1, 0), jnp.where(j == 0, 1, 2))
            flip = jnp.where(phase == 0, jnp.where(j == 2, 1, 0), jnp.where(j == 1, 0, 1))
            h = jnp.where(j < 2, u - 8 * phase, jnp.where(phase == 0, u, late))
            live = jnp.where(j < 2, u < 16, (phase == 0) | ((late >= 0) & (late < 8)))
            zz = z + flip - 2 * z * flip
            first = slot(back, 0, zz)
            mask_at = back * 2 + flip
            has0 = live & needed(back, 0, zz)
            has1 = live & needed(back, 1, zz)

            @pl.when(has0 & has1)
            def _():
                both = buf[pl.ds(first, 2), h]
                update(
                    both[:, :ROWS].reshape(2 * ROWS, D),
                    both[:, ROWS:].reshape(2 * ROWS, D),
                    masks[mask_at],
                    h,
                )

            @pl.when(jnp.logical_xor(has0, has1))
            def _():
                core = jnp.where(has1, 1, 0)
                one = buf[first + core, h]
                update(
                    one[:ROWS],
                    one[ROWS:],
                    masks[mask_at, pl.ds(pl.multiple_of(core * ROWS, ROWS), ROWS)],
                    h,
                )

    def out_copy(h):
        return pltpu.make_async_copy(
            ostage.at[h], out_hbm.at[:, pl.ds(pl.multiple_of(h * G * D, D), G * D)], out_sem.at[h]
        )

    sib = 1 - c

    @pl.loop(0, 17 + LAG)
    def _(t):
        @pl.when(t < 16)
        def _():
            phase = lax.div(t, 8)
            h = lax.rem(t, 8)
            from_above = slot(3 - phase, c, z)
            arrived(from_above, h)

            @pl.when(phase == 0)
            def _():
                send(1, from_above, h, 8 + h).start()

            @pl.when(phase == 1)
            def _():
                send(2, from_above, h, 8 + h).start()
                send(3, from_above, h, 40 + h).start()

            from_below = slot(1, c, z + phase - 2 * z * phase)
            arrived(from_below, h)
            send(3, from_below, h, 8 + t).start()

        @pl.when(t < 8)
        def _():
            block = slot(0, c, 1 - z)
            arrived(block, t)
            send(0, block, t, 8 + t).start()
            send(3, block, t, 24 + t).start()

        @pl.when((t >= 8 + LAG) & (t < 16 + LAG))
        def _():
            e = t - 8 - LAG
            block = slot(2, c, 1 - z)
            arrived(block, e)
            send(3, block, e, 32 + e).start()

        u = t - 1

        @pl.when((u >= 0) & (u < 8))
        def _():
            arrived(slot(0, sib, z), u)
            arrived(slot(1, sib, z), u)
            arrived(slot(0, sib, 1 - z), u)

        @pl.when((u >= 8) & (u < 16))
        def _():
            arrived(slot(1, sib, 1 - z), u - 8)
            arrived(slot(2, sib, z), u - 8)

        @pl.when(u >= 8 + LAG)
        def _():
            arrived(slot(2, sib, 1 - z), u - 8 - LAG)

        @pl.when(u >= 0)
        def _():
            compute(u)

        @pl.when(u >= 9 + LAG)
        def _():
            out_copy(u - 9 - LAG).start()

        @pl.when(u >= 8 + LAG)
        def _():
            e = u - 8 - LAG
            for g in range(G):
                i = e * G + g
                ostage[e, :, g * D:(g + 1) * D] = (acc[i] / total[i]).T.astype(jnp.bfloat16)

    @pl.loop(0, KH)
    def _(h):
        for link in range(4):
            send(link, own_slot, h, h).wait_send()
        send(0, own_slot, h, 8 + h).wait_send()
        send(1, own_slot, h, 8 + h).wait_send()
        send(2, own_slot, h, 8 + h).wait_send()
        for more in range(5):
            send(3, own_slot, h, 8 + 8 * more + h).wait_send()

    out_copy(KH - 1).start()

    @pl.loop(0, KH)
    def _(h):
        out_copy(h).wait()


def local(queries, keys, values, positions, doc_lengths):
    exponent = -2.0 * np.arange(HALF, dtype=np.float64) / D
    freq = np.power(1000000.0, exponent).astype(np.float32)
    freq = jnp.asarray(np.broadcast_to(freq[:, None], (HALF, ROWS)))
    any_space = pl.BlockSpec(memory_space=pl.ANY)
    vmem = pl.BlockSpec(memory_space=pltpu.VMEM)
    bf16, f32 = jnp.bfloat16, jnp.float32
    heads = KH * G
    return pl.pallas_call(
        kernel,
        out_shape=jax.ShapeDtypeStruct(queries.shape, bf16),
        in_specs=[any_space, any_space, any_space, vmem, vmem, pl.BlockSpec(memory_space=pltpu.SMEM)],
        out_specs=any_space,
        scratch_shapes=[
            pltpu.VMEM((16, KH, 2 * ROWS, D), bf16),
            pltpu.VMEM((ROWS, heads * D), bf16),
            pltpu.VMEM((heads, ROWS, D), bf16),
            pltpu.VMEM((ROWS, KH * D), bf16),
            pltpu.VMEM((heads, D, ROWS), f32),
            pltpu.VMEM((heads, 1, ROWS), f32),
            pltpu.VMEM((heads, 1, ROWS), f32),
            pltpu.VMEM((6, 2 * ROWS, ROWS), f32),
            pltpu.VMEM((ROWS, D), f32),
            pltpu.VMEM((ROWS, D), f32),
            pltpu.VMEM((KH, ROWS, G * D), bf16),
            pltpu.SemaphoreType.DMA((2,)),
            pltpu.SemaphoreType.DMA((KH,)),
            pltpu.SemaphoreType.DMA((KH,)),
            pltpu.SemaphoreType.DMA((96,)),
            pltpu.SemaphoreType.DMA((128,)),
        ],
        compiler_params=pltpu.CompilerParams(
            collective_id=0, has_side_effects=True, vmem_limit_bytes=60 * 1024 * 1024
        ),
    )(queries, keys, values, positions, freq, doc_lengths)


def solution(mesh):
    rows = ("seq", "blk", "uly")
    in_specs = (P(rows, None), P(rows, None), P(rows, None), P(None, rows), P("seq"))
    return jax.shard_map(
        local, mesh=mesh, in_specs=in_specs, out_specs=P(rows, None), check_vma=False
    )
```

time: 313 us -> 83.6 us (0.27)
  waiting for transfers between devices: 107 us -> 0 us
  matrix products: 93.6 us -> 0 us
  Pallas kernels: 0 us -> 78.7 us
  local copies, waits for them, and re-layouts: 48.9 us -> 4.76 us
  other arithmetic: 38.7 us -> 0 us
  between operations: 13.5 us -> 0.01 us
  loops' own time: 10.3 us -> 0 us
    all_gather x1 -> x0, waiting for transfers between devices: 107 us -> none  [fold_all(): lax.all_gather(paired, ('blk', 'uly'), axis=0, tiled=True)]
    dot_general x10 -> x0, matrix products: 93.6 us -> none  [the longest x5 68 us: update(): jnp.einsum('hgrb,bhd->hgrd', weights.astype(jnp.bfloat16), values_blk, pr...]
    pallas_call x0 -> x1, Pallas kernels: none -> 78.7 us  [local(): pl.pallas_call(kernel, out_shape=jax.ShapeDtypeStruct(queries.shape, bf16...]
    reduce_sum x6 -> x0, other arithmetic: 25.3 us -> none  [the longest x5 25.2 us: update(): total = total * factor + jnp.sum(weights, axis=-1)]
    slice x8 -> x0, local copies, waits for them, and re-layouts: 19.9 us -> none  [the longest x5 13.6 us: step(): values_blk = slab[:, kheads * HEAD_SIZE:].reshape(block, kheads, HEAD_SIZE)]
    cond x25 -> x0, local copies, waits for them, and re-layouts: 11.1 us -> none
    another operation x9 -> x0, loops' own time: 10.3 us -> none  [the longest x1 9.73 us: fold_piece(): return lax.fori_loop(0, count // block, step, carry)]
    while x1 -> x0, local copies, waits for them, and re-layouts: 5.9 us -> none  [fold_piece(): return lax.fori_loop(0, count // block, step, carry)]
  transfers between devices with their start and end apart: 1 -> 0, of which waited for: 1 -> 0; matrix products, arithmetic and copies ran while one was open for 5% -> 0% of each run, Pallas kernels for 0% -> 0%
where the time goes in v1:
time: 83.6 us; the launch traced here: 83.4 us
  Pallas kernels  78.7 us (94%)
  local copies, waits for them, and re-layouts  4.76 us (6%)
    pallas_call x1, Pallas kernels, local(): pl.pallas_call(kernel, out_shape=jax.ShapeDtypeStruct(queries.shape, bf16...  78.7 us
    unnamed x1, local copies, waits for them, and re-layouts  3.4 us

profile of v1, /device:TPU:28, one launch (start us, length us, event | category | flops | bytes accessed | tf_op | source)
XLA Modules:
  0.0 83.4 jit_solution(16138726036755069159)
XLA Ops:
  0.0 1.4 %jit_solution_.3.freq_ref = f32[64,256]{1,0:T(8,128)} broadcast(f32[64]{0:T(128)} %constant.2.clone), dimensions={0} | broadcast | bytes 65792 | tf_op jit(solution)
  1.4 78.7 %shard_map.64 = bf16[256,5120]{1,0:T(8,128)(2,1)} custom-call(bf16[256,5120]{1,0:T(8,128)(2,1)} %q_hbm.1, bf16[256,1024]{1,0:T(8,128)(2,1)} %k_hbm.1, bf16[256,1024]{1,0:T(8,128)(2,1)} %v_hbm.1, s32[3,256]{1,0:T(4,128)} %pos_ref.1, f32[64,256]{1,0:T(8,128)} %jit_solution_.3.freq_ref, s32[8]{0:T(128)} %docs_ref.1), custom_call_target="tpu_custom_call" | custom-call | tf_op jit(solution)/shard_map/pallas_call | solution.py:301
  80.0 3.4 %copy.8 = bf16[256,5120]{1,0:T(8,128)(2,1)} copy(bf16[256,5120]{1,0:T(8,128)(2,1)} %shard_map.64) | data formatting | bytes 5242880

commit v2 on v1

v2 whole, which is shorter than its diff:
```python
import math

import jax
import jax.numpy as jnp
from jax import lax
from jax.experimental import pallas as pl
from jax.experimental.pallas import tpu as pltpu
from jax.sharding import PartitionSpec as P

D = 128
G = 5
KH = 8
ROWS = 256
LAG = 2
AHEAD = 5
CHUNK = 16
HALF = D // 2
BIG = 3.0e38
LOW = -1.0e30
EXP_SCALE = math.log2(math.e) / math.sqrt(D)
MESH = pl.DeviceIdType.MESH
CONTRACT_LAST = (((1,), (1,)), ((), ()))
CONTRACT_FIRST = (((0,), (0,)), ((), ()))


def kernel(
    q_hbm, k_hbm, v_hbm, pos_ref, docs_ref, out_ref,
    buf, qraw, qs, kraw, acc, best, total, held, weights, masks, bias, onehot, cos_t, sin_t,
    in_sem, v_sem, send_sem, recv_sem,
):
    s = lax.axis_index("seq")
    blk = lax.axis_index("blk")
    z = lax.axis_index("uly")
    y = lax.div(blk, 2)
    c = lax.rem(blk, 2)
    own = 4 * y + 2 * c + z
    up = (s, 2 * lax.rem(y + 1, 4) + c, z)
    down = (s, 2 * lax.rem(y + 3, 4) + c, z)
    across = (s, blk, 1 - z)
    sibling = (s, 2 * y + 1 - c, z)
    links = (up, down, across, sibling)

    def slot(back, core, zz):
        return 4 * lax.rem(y + 4 - back, 4) + 2 * zz + core

    own_slot = slot(0, c, z)

    k_copy = pltpu.make_async_copy(k_hbm, kraw, in_sem.at[0])
    k_copy.start()
    v_copies = [
        pltpu.make_async_copy(
            v_hbm.at[:, h * D:(h + 1) * D], buf.at[own_slot, h, ROWS:2 * ROWS, :], v_sem.at[h]
        )
        for h in range(KH)
    ]
    for copy in v_copies:
        copy.start()
    q_copy = pltpu.make_async_copy(q_hbm, qraw, in_sem.at[1])
    q_copy.start()

    barrier = pltpu.get_barrier_semaphore()
    for peer in links:
        pl.semaphore_signal(barrier, inc=1, device_id=peer, device_id_type=MESH)

    pair = lax.broadcasted_iota(jnp.int32, (HALF, ROWS), 0)
    place = pos_ref[...].astype(jnp.float32)
    chosen = jnp.where(
        pair < D // 8,
        place[0:1, :],
        jnp.where(pair < D // 8 + 3 * D // 16, place[1:2, :], place[2:3, :]),
    )
    step = -2.0 * math.log2(1000000.0) / D
    angle = chosen * jnp.exp2(step * pair.astype(jnp.float32))
    cosine = jnp.cos(angle)
    sine = jnp.sin(angle)
    cos_t[...] = jnp.concatenate([cosine, cosine], axis=0).T
    sin_t[...] = jnp.concatenate([-sine, sine], axis=0).T

    def rotate(x):
        x = x.astype(jnp.float32)
        return (x * cos_t[...] + pltpu.roll(x, HALF, 1) * sin_t[...]).astype(jnp.bfloat16)

    k_copy.wait()
    for h in range(KH):
        buf[own_slot, h, 0:ROWS, :] = rotate(kraw[:, h * D:(h + 1) * D])
    for copy in v_copies:
        copy.wait()

    pl.semaphore_wait(barrier, 4)

    def send(link, block, h, count):
        return pltpu.make_async_remote_copy(
            src_ref=buf.at[block, h],
            dst_ref=buf.at[block, h],
            send_sem=send_sem.at[link * 16 + count],
            recv_sem=recv_sem.at[block * 8 + h],
            device_id=links[link],
            device_id_type=MESH,
        )

    def arrived(block, h):
        pltpu.make_async_copy(
            buf.at[block, h], buf.at[block, h], recv_sem.at[block * 8 + h]
        ).wait()

    @pl.loop(0, KH)
    def _(h):
        for link in range(4):
            send(link, own_slot, h, h).start()

    lane = lax.broadcasted_iota(jnp.int32, (1, D), 1)
    first_of = jnp.zeros((1, D), jnp.int32)
    end_of = jnp.zeros((1, D), jnp.int32)
    end = 0
    for d in range(8):
        first_of = jnp.where(lane == d, end, first_of)
        end = end + docs_ref[d]
        end_of = jnp.where(lane == d, end, end_of)
    row = lax.broadcasted_iota(jnp.int32, (ROWS, D), 0)
    index = row + own * ROWS
    inside = (index >= first_of) & (index < end_of)
    onehot[...] = jnp.where(inside, 1.0, 0.0).astype(jnp.bfloat16)
    for at in range(12):
        back, flip, core = at // 4, at // 2 % 2, at % 2
        zz = 1 - z if flip else z
        index = row + (4 * (y - back) + 2 * core + zz) * ROWS
        inside = ((index >= first_of) & (index < end_of)) | (lane >= 8)
        bias[at] = jnp.where(inside, 0.0, LOW).astype(jnp.bfloat16)
    key_row = lax.broadcasted_iota(jnp.int32, (ROWS, ROWS), 0)
    query_row = lax.broadcasted_iota(jnp.int32, (ROWS, ROWS), 1)
    masks[0] = jnp.where(key_row <= query_row, BIG, LOW)
    masks[1] = jnp.full((ROWS, ROWS), BIG, jnp.float32)

    acc[...] = jnp.zeros_like(acc)
    total[...] = jnp.zeros_like(total)
    best[...] = jnp.full_like(best, LOW)
    q_copy.wait()

    @pl.loop(0, KH * G)
    def _(i):
        qs[i] = rotate(qraw[:, pl.ds(pl.multiple_of(i * D, D), D)])

    def update(places, bias_at, phase, h):
        width = len(places) * ROWS
        keys = jnp.concatenate(
            [
                jnp.concatenate([buf[p, h, :ROWS, :], bias[at]], axis=1)
                for p, at in zip(places, bias_at)
            ],
            axis=0,
        )
        vals = jnp.concatenate([buf[p, h, ROWS:, :] for p in places], axis=0)
        olds = [best[h * G + g] for g in range(G)]
        sums = [total[h * G + g] for g in range(G)]
        news, factors, parts, outs = [], [], [], []

        def score(g):
            query = jnp.concatenate([qs[h * G + g], onehot[...]], axis=1)
            sc = lax.dot_general(keys, query, CONTRACT_LAST, preferred_element_type=jnp.float32)
            head = jnp.minimum(sc[:ROWS], masks[phase])
            held[g, :ROWS] = head
            held[g, ROWS:width] = sc[ROWS:]
            new = jnp.maximum(olds[g], jnp.max(head, axis=0, keepdims=True))
            new = jnp.maximum(new, jnp.max(sc[ROWS:], axis=0, keepdims=True))
            news.append(new)
            factors.append(jnp.exp2((olds[g] - new) * EXP_SCALE))

        def soften(g):
            level = news[g] * EXP_SCALE
            part = jnp.zeros((8, ROWS), jnp.float32)
            for at in range(0, width, CHUNK):
                w = jnp.exp2(held[g, at:at + CHUNK] * EXP_SCALE - level)
                for row in range(0, CHUNK, 8):
                    part = part + w[row:row + 8]
                weights[g, at:at + CHUNK] = w.astype(jnp.bfloat16)
            parts.append(jnp.sum(part, axis=0, keepdims=True))

        def gather(g):
            outs.append(
                lax.dot_general(
                    vals, weights[g, :width], CONTRACT_FIRST, preferred_element_type=jnp.float32
                )
            )

        for g in range(AHEAD):
            score(g)
        for g in range(G):
            if g + AHEAD < G:
                score(g + AHEAD)
            soften(g)
            gather(g)
        for g in range(G):
            i = h * G + g
            best[i] = news[g]
            total[i] = sums[g] * factors[g] + parts[g]
            acc[i] = acc[i] * factors[g] + outs[g]

    rank = 2 * c + z

    def early_blocks(r):
        blocks = [(0, 0, r // 2), (1, 0, 0), (1, 0, 1)]
        for core in range(2):
            for flip in range(2):
                if 2 * core + ((r % 2) ^ flip) < r:
                    blocks.append((0, flip, core))
        return blocks

    def late_blocks(r):
        blocks = [(1, 1, 0), (1, 1, 1)]
        for flip in range(2):
            for core in range(2):
                if 2 * core + ((r % 2) ^ flip) >= r:
                    blocks.append((2, flip, core))
        return blocks

    def compute(phase, h):
        for count in range(3, 7):
            early, late = early_blocks(count - 3), late_blocks(6 - count)
            assert len(early) == count and len(late) == count

            @pl.when(rank == jnp.where(phase == 0, count - 3, 6 - count))
            def _():
                def place(b):
                    back, flip, core = b
                    return slot(back, core, 1 - z if flip else z)

                def bias_of(b):
                    return 4 * b[0] + 2 * b[1] + b[2]

                update(
                    [jnp.where(phase == 0, place(e), place(f)) for e, f in zip(early, late)],
                    [jnp.where(phase == 0, bias_of(e), bias_of(f)) for e, f in zip(early, late)],
                    phase,
                    h,
                )

    sib = 1 - c

    @pl.loop(0, 17 + LAG)
    def _(t):
        @pl.when(t < 16)
        def _():
            phase = lax.div(t, 8)
            h = lax.rem(t, 8)
            from_above = slot(3 - phase, c, z)
            arrived(from_above, h)

            @pl.when(phase == 0)
            def _():
                send(1, from_above, h, 8 + h).start()

            @pl.when(phase == 1)
            def _():
                send(2, from_above, h, 8 + h).start()
                send(3, from_above, h, 40 + h).start()

            from_below = slot(1, c, z + phase - 2 * z * phase)
            arrived(from_below, h)
            send(3, from_below, h, 8 + t).start()

        @pl.when(t < 8)
        def _():
            block = slot(0, c, 1 - z)
            arrived(block, t)
            send(0, block, t, 8 + t).start()
            send(3, block, t, 24 + t).start()

        @pl.when((t >= 8 + LAG) & (t < 16 + LAG))
        def _():
            e = t - 8 - LAG
            block = slot(2, c, 1 - z)
            arrived(block, e)
            send(3, block, e, 32 + e).start()

        u = t - 1

        @pl.when((u >= 0) & (u < 8))
        def _():
            arrived(slot(0, sib, z), u)
            arrived(slot(1, sib, z), u)
            arrived(slot(0, sib, 1 - z), u)

        @pl.when((u >= 8) & (u < 16))
        def _():
            arrived(slot(1, sib, 1 - z), u - 8)
            arrived(slot(2, sib, z), u - 8)

        @pl.when(u >= 8 + LAG)
        def _():
            arrived(slot(2, sib, 1 - z), u - 8 - LAG)

        late = u - 8 - LAG

        @pl.when(((u >= 0) & (u < 8)) | (late >= 0))
        def _():
            compute(jnp.where(late >= 0, 1, 0), jnp.where(late >= 0, late, u))

        @pl.when(u >= 8 + LAG)
        def _():
            e = u - 8 - LAG
            for g in range(G):
                i = e * G + g
                out_ref[:, pl.ds(pl.multiple_of(i * D, D), D)] = (
                    (acc[i] / total[i]).T.astype(jnp.bfloat16)
                )

    @pl.loop(0, KH)
    def _(h):
        for link in range(4):
            send(link, own_slot, h, h).wait_send()
        send(0, own_slot, h, 8 + h).wait_send()
        send(1, own_slot, h, 8 + h).wait_send()
        send(2, own_slot, h, 8 + h).wait_send()
        for more in range(5):
            send(3, own_slot, h, 8 + 8 * more + h).wait_send()


def local(queries, keys, values, positions, doc_lengths):
    any_space = pl.BlockSpec(memory_space=pl.ANY)
    vmem = pl.BlockSpec(memory_space=pltpu.VMEM)
    bf16, f32 = jnp.bfloat16, jnp.float32
    heads = KH * G
    return pl.pallas_call(
        kernel,
        out_shape=pltpu.VMEM(queries.shape, bf16),
        in_specs=[any_space, any_space, any_space, vmem, pl.BlockSpec(memory_space=pltpu.SMEM)],
        out_specs=vmem,
        scratch_shapes=[
            pltpu.VMEM((16, KH, 2 * ROWS, D), bf16),
            pltpu.VMEM((ROWS, heads * D), bf16),
            pltpu.VMEM((heads, ROWS, D), bf16),
            pltpu.VMEM((ROWS, KH * D), bf16),
            pltpu.VMEM((heads, D, ROWS), f32),
            pltpu.VMEM((heads, 1, ROWS), f32),
            pltpu.VMEM((heads, 1, ROWS), f32),
            pltpu.VMEM((G, 6 * ROWS, ROWS), f32),
            pltpu.VMEM((G, 6 * ROWS, ROWS), bf16),
            pltpu.VMEM((2, ROWS, ROWS), f32),
            pltpu.VMEM((12, ROWS, D), bf16),
            pltpu.VMEM((ROWS, D), bf16),
            pltpu.VMEM((ROWS, D), f32),
            pltpu.VMEM((ROWS, D), f32),
            pltpu.SemaphoreType.DMA((2,)),
            pltpu.SemaphoreType.DMA((KH,)),
            pltpu.SemaphoreType.DMA((96,)),
            pltpu.SemaphoreType.DMA((128,)),
        ],
        compiler_params=pltpu.CompilerParams(
            collective_id=0, has_side_effects=True, vmem_limit_bytes=56 * 1024 * 1024
        ),
    )(queries, keys, values, positions, doc_lengths)


def solution(mesh):
    rows = ("seq", "blk", "uly")
    in_specs = (P(rows, None), P(rows, None), P(rows, None), P(None, rows), P("seq"))
    return jax.shard_map(
        local, mesh=mesh, in_specs=in_specs, out_specs=P(rows, None), check_vma=False
    )
```

time: 83.6 us -> 72.2 us (0.86); the launches traced: 83.4 us -> 70.9 us
  Pallas kernels: 78.7 us -> 69.4 us
  local copies, waits for them, and re-layouts: 4.76 us -> 1.49 us
    pallas_call x1, Pallas kernels: 78.7 us -> 69.4 us  [local(): pl.pallas_call(kernel, out_shape=pltpu.VMEM(queries.shape, bf16), in_spec...]
    unnamed x1, local copies, waits for them, and re-layouts: 3.4 us -> 1.49 us
    another operation x1 -> x0, local copies, waits for them, and re-layouts: 1.36 us -> none
where the time goes in v2:
time: 72.2 us; the launch traced here: 70.9 us
  Pallas kernels  69.4 us (96%)
  local copies, waits for them, and re-layouts  1.49 us (2%)
    pallas_call x1, Pallas kernels, local(): pl.pallas_call(kernel, out_shape=pltpu.VMEM(queries.shape, bf16), in_spec...  69.4 us
    unnamed x1, local copies, waits for them, and re-layouts  1.49 us

profile of v2, /device:TPU:28, one launch (start us, length us, event | category | flops | bytes accessed | tf_op | source)
XLA Modules:
  0.0 70.9 jit_solution(6562953032691620725)
XLA Ops:
  0.0 69.4 %shard_map.55 = bf16[256,5120]{1,0:T(8,128)(2,1)S(1)} custom-call(bf16[256,5120]{1,0:T(8,128)(2,1)} %q_hbm.1, bf16[256,1024]{1,0:T(8,128)(2,1)} %k_hbm.1, bf16[256,1024]{1,0:T(8,128)(2,1)} %v_hbm.1, s32[3,256]{1,0:T(4,128)} %pos_ref.1, s32[8]{0:T(128)} %docs_ref.1), custom_call_target="tpu_custom_call" | custom-call | tf_op jit(solution)/shard_map/pallas_call | solution.py:323
  69.4 1.5 %copy.7 = bf16[256,5120]{1,0:T(8,128)(2,1)} copy(bf16[256,5120]{1,0:T(8,128)(2,1)S(1)} %shard_map.55) | data formatting | bytes 5242880
